TPU v7x, 256 devices: a whole 4x4x8 slice. The times are simulated.
256 devices in a mesh: seq: 16 (over z, core), tp: 8 (over x_lo, y), dp: 2 (over x_hi).
Axes of the slice: x: 4 (x_hi: 2, x_lo: 2; x = x_hi * 2 + x_lo), y: 4, z: 8, core: 2. Of those that a mesh axis runs over, the one named last changes fastest.
Arguments:
- query_latent: bfloat16 [2, 4096, 1536], P('dp', 'seq', 'tp'), may hold values from -6 to 6
- key_latent: bfloat16 [2, 4096, 512], P('dp', 'seq', 'tp'), may hold values from -6 to 6
- rope_key: bfloat16 [2, 4096, 64], P('dp', 'seq'), may hold values from -6 to 6
- w_uq: bfloat16 [1536, 12288], P('seq', 'tp')
- w_uk: bfloat16 [512, 8192], P('seq', 'tp'), may hold values from -0.25 to 0.25
- w_uv: bfloat16 [512, 8192], P('seq', 'tp'), may hold values from -0.25 to 0.25
- block_order: int32 [2, 32], P('dp'), may hold values from 0 to 31, each once within a row
- segment_ids: int32 [2, 4096], P('dp'), may hold values from 0 to 3, never falling along the last dimension, each value on 1 to 2048 neighbouring positions
Outputs:
- context: bfloat16 [2, 4096, 8192], P('dp', 'seq', 'tp')
- clipped_uq: bfloat16 [1536, 12288], P('seq', 'tp')
- clipped_uk: bfloat16 [512, 8192], P('seq', 'tp')
Inputs may be any that keep to these rules, and one draw needn't show every extreme that they name: `block_order`: each row is a permutation of the 32 position blocks. `segment_ids`: never falling along positions; each document has at most 2048 positions.
All inputs are finite; a program needn't handle non-finite values.
Results may differ from a plain program's by a relative error of at most 0.012.
The roundings to bfloat16 on the way count: a program that leaves them out, or rounds other values in their place, can miss the bound.
Values may be sent and summed in bfloat16 or wider, within the bound.
A program may use at most 64 MiB of HBM per device.

v0:
```python
import math
import jax
import jax.numpy as jnp
from jax import lax
from jax.sharding import PartitionSpec as P

NOPE = 128
ROPE = 64
VD = 128
CLIP = 8
rope_base = 50000.0
masked_value = -1e30


def in_one_piece(arrays, axis, dim, along):
    both = jnp.concatenate(arrays, axis=along)
    whole, at, gathered = (lax.all_gather(both, axis, axis=dim, tiled=True), 0, [])
    for a in arrays:
        gathered.append(lax.slice_in_dim(whole, at, at + a.shape[along], axis=along))
        at += a.shape[along]
    return tuple(gathered)


def copy_for_each(array, axis):
    copies = jnp.broadcast_to(array, (lax.axis_size(axis), *array.shape))
    return lax.all_to_all(copies, axis, split_axis=0, concat_axis=0, tiled=True)


def of_everyone(array, axis):
    everything = copy_for_each(array, axis)
    return jnp.max(everything, axis=0)


def turning(positions, width):
    steps = jnp.arange(width // 2, dtype=jnp.float32) * (2.0 / width)
    freqs = jnp.exp(-math.log(rope_base) * steps)
    angle = positions.astype(jnp.float32)[:, None] * freqs[None, :]
    return (jnp.cos(angle), jnp.sin(angle))


def rotate(values, cosine, sine):
    half = values.shape[-1] // 2
    first = values[..., :half]
    second = values[..., half:]
    return jnp.concatenate(
        [first * cosine - second * sine, second * cosine + first * sine], axis=-1
    )


def positions_of(index, order, half_block):
    which = index // half_block
    onehot = which[:, None] == jnp.arange(order.shape[0], dtype=jnp.int32)[None, :]
    base = jnp.sum(jnp.where(onehot, order[None, :], 0), axis=1)
    return base * half_block + index % half_block


def on_device(query_latent, key_latent, rope_key, w_uq, w_uk, w_uv, block_order, segment_ids):
    query_local, key_local = (
        lax.all_gather(query_latent[0], "tp", axis=1, tiled=True),
        lax.all_gather(key_latent[0], "tp", axis=1, tiled=True),
    )
    rows_uq, rows_uk, rows_uv = (
        lax.all_gather(w_uq, "seq", axis=0, tiled=True),
        *in_one_piece((w_uk, w_uv), "seq", 0, 1),
    )
    tok_rows = query_local.shape[0]
    half_block = tok_rows // 2
    order = block_order[0]
    labels_all = segment_ids[0]
    heads = w_uq.shape[1] // (NOPE + ROPE)
    scale = 1.0 / math.sqrt(NOPE + ROPE)
    own_index = lax.axis_index("seq") * tok_rows + jnp.arange(tok_rows, dtype=jnp.int32)
    query_pos = positions_of(own_index, order, half_block)
    query_labels = jnp.take(labels_all, query_pos)
    cosine, sine = turning(query_pos, ROPE)
    query_full = jnp.dot(query_local, rows_uq, preferred_element_type=jnp.float32).reshape(
        tok_rows, heads, NOPE + ROPE
    )
    query_nope = jnp.transpose(query_full[:, :, :NOPE].astype(jnp.bfloat16), (1, 0, 2))
    query_rope = jnp.transpose(
        rotate(query_full[:, :, NOPE:], cosine[:, None, :], sine[:, None, :]).astype(jnp.bfloat16),
        (1, 0, 2),
    )
    key_rope = rotate(rope_key[0].astype(jnp.float32), cosine, sine).astype(jnp.bfloat16)

    def slice_latent(pieces, first, width):
        latent_block = lax.dynamic_slice_in_dim(pieces[0], first, width, 0)
        rope_block = lax.dynamic_slice_in_dim(pieces[1], first, width, 0)
        nope_block = jnp.dot(latent_block, rows_uk, preferred_element_type=jnp.float32).astype(
            jnp.bfloat16
        )
        value_block = jnp.dot(latent_block, rows_uv, preferred_element_type=jnp.float32).astype(
            jnp.bfloat16
        )
        return (nope_block, value_block, rope_block)

    initial = (
        jnp.full((heads, tok_rows), masked_value, jnp.float32),
        jnp.zeros((heads, tok_rows), jnp.float32),
        jnp.zeros((heads, tok_rows, VD), jnp.float32),
    )
    pieces = in_one_piece((key_local, key_rope), "seq", 0, 1)
    count = pieces[-1].shape[0]
    width = math.gcd(count, 512)

    def block_step(state, number):
        first = number * width
        nope_block, value_block, rope_block = slice_latent(pieces, first, width)
        nope_block = nope_block.reshape(width, heads, NOPE)
        value_block = value_block.reshape(width, heads, VD)
        key_index = first + jnp.arange(width, dtype=jnp.int32)
        key_pos = positions_of(key_index, order, half_block)
        key_labels = jnp.take(labels_all, key_pos)
        allowed = (key_pos[None, :] <= query_pos[:, None]) & (
            key_labels[None, :] == query_labels[:, None]
        )
        scores = jnp.einsum(
            "hqd,khd->hqk", query_nope, nope_block, preferred_element_type=jnp.float32
        )
        scores = (
            scores
            + jnp.einsum("hqr,kr->hqk", query_rope, rope_block, preferred_element_type=jnp.float32)
        ) * scale
        masked = jnp.where(allowed[None], scores, masked_value)
        run_max, run_total, run_sum = state
        new_max = jnp.maximum(run_max, jnp.max(masked, axis=2))
        weights = jnp.where(allowed[None], jnp.exp(masked - new_max[:, :, None]), 0.0)
        shrink = jnp.exp(run_max - new_max)
        new_total = run_total * shrink + jnp.sum(weights, axis=2)
        mixed = jnp.einsum(
            "hqk,khv->hqv",
            weights.astype(jnp.bfloat16),
            value_block,
            preferred_element_type=jnp.float32,
        )
        new_sum = run_sum * shrink[:, :, None] + mixed
        return ((new_max, new_total, new_sum), None)

    result, unused = lax.scan(block_step, initial, jnp.arange(count // width, dtype=jnp.int32))
    run_max, run_total, run_sum = result
    context = (run_sum / run_total[:, :, None]).astype(jnp.bfloat16)
    context = jnp.transpose(context, (1, 0, 2)).reshape(1, tok_rows, heads * VD)
    head_max = of_everyone(jnp.max(run_max, axis=1), ("seq", "dp"))
    ratio = CLIP / jnp.maximum(head_max, CLIP)
    root = jnp.sqrt(ratio)
    factors = jnp.concatenate(
        [
            jnp.broadcast_to(root[:, None], (heads, NOPE)),
            jnp.broadcast_to(ratio[:, None], (heads, ROPE)),
        ],
        axis=1,
    ).reshape(heads * (NOPE + ROPE))
    clipped_uq = (w_uq.astype(jnp.float32) * factors[None, :]).astype(jnp.bfloat16)
    clipped_uk = (w_uk.astype(jnp.float32) * jnp.repeat(root, NOPE)[None, :]).astype(jnp.bfloat16)
    return (context, clipped_uq, clipped_uk)


def solution(mesh):
    placed = (
        P("dp", "seq", "tp"),
        P("dp", "seq", "tp"),
        P("dp", "seq", None),
        P("seq", "tp"),
        P("seq", "tp"),
        P("seq", "tp"),
        P("dp", None),
        P("dp", None),
    )
    return jax.shard_map(
        on_device,
        mesh=mesh,
        in_specs=placed,
        out_specs=(P("dp", "seq", "tp"), P("seq", "tp"), P("seq", "tp")),
        check_vma=False,
    )
```

profile of v0, /device:TPU:1, one launch (start us, length us, event | category | flops | bytes accessed | tf_op | source)
XLA Modules:
  0.0 318.9 jit_solution(3619751761167049649)
XLA Ops:
  10.4 24.1 %all-gather = bf16[1,256,512]{1,2,0:T(8,128)(2,1)S(1)} all-gather(bf16[1,256,64]{1,2,0:T(8,128)(2,1)} %param.11), channel_id=2, replica_groups=mesh['seq'=16,'tp'=8,'dp'=2] {'tp'}, dimensions={2}, use_global_device_ids=true | all-gather | bytes 294912 | tf_op jit(solution)/shard_map/all_gather | solution.py:60
  38.2 24.7 %all-gather.1 = bf16[1,256,1536]{1,2,0:T(8,128)(2,1)S(1)} all-gather(bf16[1,256,192]{1,2,0:T(8,128)(2,1)} %param.10), channel_id=3, replica_groups=mesh['seq'=16,'tp'=8,'dp'=2] {'tp'}, dimensions={2}, use_global_device_ids=true | all-gather | bytes 884736 | tf_op jit(solution)/shard_map/all_gather | solution.py:59
  62.9 3.2 fusion.47
  66.0 30.5 %all-gather.10.cloned.1.call-done = bf16[1536,1536]{1,0:T(8,128)(2,1)} async-done(((bf16[96,1536]{1,0:T(8,128)(2,1)}), bf16[1536,1536]{1,0:T(8,128)(2,1)}) %all-gather.10.cloned.1.call-update) | async-done | bytes 4718608 | tf_op jit(solution)/shard_map/all_gather | solution.py:63
  96.5 4.3 %fusion.34 = f32[256,1536]{0,1:T(8,128)S(1)} fusion(bf16[1536,1536]{1,0:T(8,128)(2,1)} %all-gather.10.cloned.1.call-done, bf16[1,256,1536]{1,2,0:T(8,128)(2,1)S(1)} %all-gather.1), kind=kOutput, calls=%fused_computation.61 | convolution fusion | flops 1207959552 | bytes 7077888 | tf_op jit(solution)/shard_map/dot_general | solution.py:76
  103.5 46.1 %all-gather.6.cloned.1.call-done = bf16[4096,576]{0,1:T(8,128)(2,1)} async-done(((bf16[256,576]{0,1:T(8,128)(2,1)}), bf16[4096,576]{0,1:T(8,128)(2,1)}) %all-gather.6.cloned.1.call-update) | async-done | bytes 4718608 | tf_op jit(solution)/shard_map/all_gather | solution.py:17
  149.6 4.8 %slice.46 = bf16[4096,512]{0,1:T(8,128)(2,1)} slice(bf16[4096,576]{0,1:T(8,128)(2,1)} %all-gather.6.cloned.1.call-done), slice={[0:4096], [0:512]} | slice | bytes 8388608 | tf_op jit(solution)/shard_map/slice | solution.py:19
  154.4 139.5 %while.17 = (s32[]{:T(128)}, f32[8,256]{1,0:T(8,128)S(1)}, f32[8,256]{1,0:T(8,128)S(1)}, f32[8,256,128]{2,1,0:T(8,128)S(1)}, s32[8]{0:T(128)S(1)}, /*index=5*/s3...) while((s32[]{:T(128)}, f32[8,256]{1,0:T(8,128)S(1)}, ...), condition=%wide.region_5.6_spmd.clone, body=%wide.region_1.5_spmd.clone.sunk | while | flops 1757632000 | bytes 48734628 | solution.py:139
  155.8 3.1 gather_fusion
  162.0 3.0 fusion.80
  165.0 3.1 fusion.81
  173.2 3.1 gather_fusion
  179.5 3.0 fusion.80
  182.4 3.1 fusion.81
  190.7 3.1 gather_fusion
  196.9 3.0 fusion.80
  199.9 3.1 fusion.81
  208.1 3.1 gather_fusion
  214.3 3.0 fusion.80
  217.3 3.1 fusion.81
  225.6 3.1 gather_fusion
  231.8 3.0 fusion.80
  234.8 3.1 fusion.81
  243.0 3.1 gather_fusion
  249.2 3.0 fusion.80
  252.2 3.1 fusion.81
  260.4 3.1 gather_fusion
  269.6 3.1 fusion.81
  277.9 3.1 gather_fusion
  287.1 3.1 fusion.81
  294.7 6.6 %all-to-all-start = ((f32[32,1,8]{2,1,0:T(1,128)}), f32[32,1,8]{2,1,0:T(1,128)S(1)}, u32[]{:S(2)}, u32[]{:S(2)}) async-start(f32[32,1,8]{2,1,0:T(1,128)} %broadcast_in_dim.126), calls=%async_computation | async-start | bytes 32768 | tf_op jit(solution)/shard_map/all_to_all | solution.py:26
  303.0 7.6 %all-to-all-done = f32[32,1,8]{2,1,0:T(1,128)S(1)} async-done(((f32[32,1,8]{2,1,0:T(1,128)}), f32[32,1,8]{2,1,0:T(1,128)S(1)}, u32[]{:S(2)}, u32[]{:S(2)}) %all-to-all-start) | async-done | bytes 1056 | tf_op jit(solution)/shard_map/all_to_all | solution.py:26
  (191 shorter events, 79.6 us)
Async XLA Ops:
  7.2 55.7 %all-gather.8.cloned.1.call-start = ((), (), s32[]{:S(2)}) async-start(), calls=%async_computation.2 | async-start | bytes 2228224 | tf_op jit(solution)/shard_map/all_gather | solution.py:17
  8.8 87.7 %all-gather.10.cloned.1.call-start = ((), (), s32[]{:S(2)}) async-start(), calls=%async_computation.3 | async-start | bytes 5013504 | tf_op jit(solution)/shard_map/all_gather | solution.py:63
  9.5 140.1 %all-gather.6.cloned.1.call-start = ((), (), s32[]{:S(2)}) async-start(), calls=%async_computation.1 | async-start | bytes 5013504 | tf_op jit(solution)/shard_map/all_gather | solution.py:17
  100.8 1.2 copy-start.3
  103.4 50.9 %copy-start = (s32[1,4096]{1,0:T(1,128)S(1)}, s32[1,4096]{1,0:T(1,128)}, u32[]{:S(2)}) copy-start(s32[1,4096]{1,0:T(1,128)} %param.17) | copy-start | bytes 49156
  103.4 50.9 %copy-start.5 = (s32[1,32]{1,0:T(1,128)S(1)}, s32[1,32]{1,0:T(1,128)}, u32[]{:S(2)}) copy-start(s32[1,32]{1,0:T(1,128)} %param.16) | copy-start | bytes 388
  149.6 4.8 %slice-start = ((bf16[4096,576]{0,1:T(8,128)(2,1)}), bf16[4096,64]{0,1:T(8,128)(2,1)S(1)}, s32[]{:S(2)}) async-start(bf16[4096,576]{0,1:T(8,128)(2,1)} %all-gather.6.cloned.1.call-done), calls=%async_computation.4 | async-start | bytes 1048576 | tf_op jit(solution)/shard_map/slice | solution.py:19
  154.4 156.6 %copy-start.2 = (bf16[96,1536]{1,0:T(8,128)(2,1)S(1)}, bf16[96,1536]{1,0:T(8,128)(2,1)}, u32[]{:S(2)}) copy-start(bf16[96,1536]{1,0:T(8,128)(2,1)} %param.13) | copy-start | bytes 884740
  165.0 5.2 %copy-start.1 = (f32[8,256,512]{1,2,0:T(8,128)S(1)}, f32[8,256,512]{1,2,0:T(8,128)}, u32[]{:S(2)}) copy-start(f32[8,256,512]{1,2,0:T(8,128)} %get-tuple-element.455) | copy-start | bytes 12582916 | tf_op jit(solution)/shard_map/while
  182.4 5.2 %copy-start.1 = (f32[8,256,512]{1,2,0:T(8,128)S(1)}, f32[8,256,512]{1,2,0:T(8,128)}, u32[]{:S(2)}) copy-start(f32[8,256,512]{1,2,0:T(8,128)} %get-tuple-element.455) | copy-start | bytes 12582916 | tf_op jit(solution)/shard_map/while
  199.9 5.2 %copy-start.1 = (f32[8,256,512]{1,2,0:T(8,128)S(1)}, f32[8,256,512]{1,2,0:T(8,128)}, u32[]{:S(2)}) copy-start(f32[8,256,512]{1,2,0:T(8,128)} %get-tuple-element.455) | copy-start | bytes 12582916 | tf_op jit(solution)/shard_map/while
  217.3 5.2 %copy-start.1 = (f32[8,256,512]{1,2,0:T(8,128)S(1)}, f32[8,256,512]{1,2,0:T(8,128)}, u32[]{:S(2)}) copy-start(f32[8,256,512]{1,2,0:T(8,128)} %get-tuple-element.455) | copy-start | bytes 12582916 | tf_op jit(solution)/shard_map/while
  234.8 5.2 %copy-start.1 = (f32[8,256,512]{1,2,0:T(8,128)S(1)}, f32[8,256,512]{1,2,0:T(8,128)}, u32[]{:S(2)}) copy-start(f32[8,256,512]{1,2,0:T(8,128)} %get-tuple-element.455) | copy-start | bytes 12582916 | tf_op jit(solution)/shard_map/while
  252.2 5.2 %copy-start.1 = (f32[8,256,512]{1,2,0:T(8,128)S(1)}, f32[8,256,512]{1,2,0:T(8,128)}, u32[]{:S(2)}) copy-start(f32[8,256,512]{1,2,0:T(8,128)} %get-tuple-element.455) | copy-start | bytes 12582916 | tf_op jit(solution)/shard_map/while
  269.6 5.2 %copy-start.1 = (f32[8,256,512]{1,2,0:T(8,128)S(1)}, f32[8,256,512]{1,2,0:T(8,128)}, u32[]{:S(2)}) copy-start(f32[8,256,512]{1,2,0:T(8,128)} %get-tuple-element.455) | copy-start | bytes 12582916 | tf_op jit(solution)/shard_map/while
  287.1 5.2 %copy-start.1 = (f32[8,256,512]{1,2,0:T(8,128)S(1)}, f32[8,256,512]{1,2,0:T(8,128)}, u32[]{:S(2)}) copy-start(f32[8,256,512]{1,2,0:T(8,128)} %get-tuple-element.455) | copy-start | bytes 12582916 | tf_op jit(solution)/shard_map/while
  293.9 17.8 %copy-start.4 = (bf16[32,1024]{1,0:T(8,128)(2,1)S(1)}, bf16[32,1024]{1,0:T(8,128)(2,1)}, u32[]{:S(2)}) copy-start(bf16[32,1024]{1,0:T(8,128)(2,1)} %param.14) | copy-start | bytes 196612
  294.7 15.9 %all-to-all-start = ((f32[32,1,8]{2,1,0:T(1,128)}), f32[32,1,8]{2,1,0:T(1,128)S(1)}, u32[]{:S(2)}, u32[]{:S(2)}) async-start(f32[32,1,8]{2,1,0:T(1,128)} %broadcast_in_dim.126), calls=%async_computation | async-start | bytes 32768 | tf_op jit(solution)/shard_map/all_to_all | solution.py:26
Sparse Core Ops, SparseCore 0:
  10.4 43.6 all-gather.7
  55.9 40.5 all-gather.9
  98.8 50.7 all-gather.5
where the time goes:
time: 320 us; the launch traced here: 319 us
  waiting for transfers between devices  84.9 us (27%)
  matrix products  80.3 us (25%)
  blocking collectives  48.7 us (15%)
  local copies, waits for them, and re-layouts  43.6 us (14%)
  other arithmetic  34.6 us (11%)
  between operations  13.9 us (4%)
  starting transfers between devices  6.74 us (2%)
  loops' own time  6.11 us (2%)
    all_gather x2, waiting for transfers between devices, in_one_piece(): lax.all_gather(both, axis, axis=dim, tiled=True)  46.1 us
    all_gather x1, waiting for transfers between devices, on_device(): lax.all_gather(w_uq, 'seq', axis=0, tiled=True)  30.5 us
    gather x8, local copies, waits for them, and re-layouts, block_step(): key_labels = jnp.take(labels_all, key_pos)  25.1 us
    all_gather x1, blocking collectives, on_device(): lax.all_gather(query_latent[0], 'tp', axis=1, tiled=True)  24.7 us
    reduce_sum x8, other arithmetic, block_step(): new_total = run_total * shrink + jnp.sum(weights, axis=2)  24.5 us
    all_gather x1, blocking collectives, on_device(): lax.all_gather(key_latent[0], 'tp', axis=1, tiled=True)  24.1 us
    dot_general x8, matrix products, block_step(): jnp.einsum('hqr,kr->hqk', query_rope, rope_block, preferred_element_type=...  23.8 us
    dot_general x8, matrix products, slice_latent(): jnp.dot(latent_block, rows_uv, preferred_element_type=jnp.float32)  17 us
  transfers between devices with their start and end apart: 4, of which 3 were waited for; matrix products, arithmetic and copies ran while one was open for 5% of the time, Pallas kernels for 0%

commit v1 on v0

--- a/solution.py
+++ b/solution.py
@@ -10,6 +10,11 @@
 CLIP = 8
 rope_base = 50000.0
 masked_value = -1e30
+
+
+def gather_by_exchange(x, axis, dim):
+    copies = jnp.concatenate([x] * lax.axis_size(axis), axis=dim)
+    return lax.all_to_all(copies, axis, dim, dim, tiled=True)
 
 
 def in_one_piece(arrays, axis, dim, along):
@@ -60,7 +65,7 @@
         lax.all_gather(key_latent[0], "tp", axis=1, tiled=True),
     )
     rows_uq, rows_uk, rows_uv = (
-        lax.all_gather(w_uq, "seq", axis=0, tiled=True),
+        gather_by_exchange(w_uq, "seq", 0),
         *in_one_piece((w_uk, w_uv), "seq", 0, 1),
     )
     tok_rows = query_local.shape[0]

time: 320 us -> 344 us (1.075)
  starting transfers between devices: 6.74 us -> 17.4 us
  local copies, waits for them, and re-layouts: 43.6 us -> 52.5 us
    all_to_all x0 -> x1, waiting for transfers between devices: none -> 59.6 us  [gather_by_exchange(): return lax.all_to_all(copies, axis, dim, dim, tiled=True)]
    all_gather x1 -> x0, waiting for transfers between devices: 30.5 us -> none  [on_device(): lax.all_gather(w_uq, 'seq', axis=0, tiled=True)]
    all_gather x2, waiting for transfers between devices: 46.1 us -> 20.6 us  [in_one_piece(): lax.all_gather(both, axis, axis=dim, tiled=True)]
    all_to_all x0 -> x1, starting transfers between devices: none -> 10.1 us  [gather_by_exchange(): return lax.all_to_all(copies, axis, dim, dim, tiled=True)]
    unnamed x11 -> x34, local copies, waits for them, and re-layouts: 1.46 us -> 10.7 us
  transfers between devices with their start and end apart: 4 -> 4, of which waited for: 3 -> 4; matrix products, arithmetic and copies ran while one was open for 5% -> 6% of each run, Pallas kernels for 0% -> 0%
where the time goes in v1:
time: 344 us; the launch traced here: 343 us
  waiting for transfers between devices  87.8 us (26%)
  matrix products  79.8 us (23%)
  local copies, waits for them, and re-layouts  52.5 us (15%)
  blocking collectives  51.4 us (15%)
  other arithmetic  33.2 us (10%)
  starting transfers between devices  17.4 us (5%)
  between operations  14.4 us (4%)
  loops' own time  6.1 us (2%)
    all_to_all x1, waiting for transfers between devices, gather_by_exchange(): return lax.all_to_all(copies, axis, dim, dim, tiled=True)  59.6 us
    all_gather x1, blocking collectives, on_device(): lax.all_gather(query_latent[0], 'tp', axis=1, tiled=True)  26 us
    all_gather x1, blocking collectives, on_device(): lax.all_gather(key_latent[0], 'tp', axis=1, tiled=True)  25.4 us
    gather x8, local copies, waits for them, and re-layouts, block_step(): key_labels = jnp.take(labels_all, key_pos)  25.1 us
    reduce_sum x8, other arithmetic, block_step(): new_total = run_total * shrink + jnp.sum(weights, axis=2)  24.5 us
    dot_general x8, matrix products, block_step(): jnp.einsum('hqr,kr->hqk', query_rope, rope_block, preferred_element_type=...  23.8 us
    all_gather x2, waiting for transfers between devices, in_one_piece(): lax.all_gather(both, axis, axis=dim, tiled=True)  20.6 us
    dot_general x8, matrix products, slice_latent(): jnp.dot(latent_block, rows_uv, preferred_element_type=jnp.float32)  17 us
  transfers between devices with their start and end apart: 4, of which 4 were waited for; matrix products, arithmetic and copies ran while one was open for 6% of the time, Pallas kernels for 0%

profile of v1, /device:TPU:1, one launch (start us, length us, event | category | flops | bytes accessed | tf_op | source)
XLA Modules:
  0.0 342.7 jit_solution(14988081886214848970)
XLA Ops:
  18.2 10.1 %all-to-all-start = ((bf16[16,96,1536]{2,1,0:T(8,128)(2,1)}), bf16[16,96,1536]{2,1,0:T(8,128)(2,1)}, u32[]{:S(2)}, u32[]{:S(2)}) async-start(bf16[16,96,1536]{2,1,0:T(8,128)(2,1)} %bitcast.84), calls=%async_computation | async-start | bytes 9437184 | tf_op jit(solution)/shard_map/all_to_all | solution.py:17
  28.5 25.4 %all-gather = bf16[1,256,512]{1,2,0:T(8,128)(2,1)S(1)} all-gather(bf16[1,256,64]{1,2,0:T(8,128)(2,1)S(1)} %copy-done.7), channel_id=2, replica_groups=mesh['seq'=16,'tp'=8,'dp'=2] {'tp'}, dimensions={2}, use_global_device_ids=true | all-gather | bytes 294912 | tf_op jit(solution)/shard_map/all_gather | solution.py:65
  56.8 26.0 %all-gather.1 = bf16[1,256,1536]{1,2,0:T(8,128)(2,1)S(1)} all-gather(bf16[1,256,192]{1,2,0:T(8,128)(2,1)S(1)} %copy-done.6), channel_id=3, replica_groups=mesh['seq'=16,'tp'=8,'dp'=2] {'tp'}, dimensions={2}, use_global_device_ids=true | all-gather | bytes 884736 | tf_op jit(solution)/shard_map/all_gather | solution.py:64
  82.8 5.4 %all-gather.7.cloned.1.call-done = bf16[512,2048]{1,0:T(8,128)(2,1)} async-done(((bf16[32,2048]{1,0:T(8,128)(2,1)}), bf16[512,2048]{1,0:T(8,128)(2,1)}) %all-gather.7.cloned.1.call-update) | async-done | bytes 2097168 | tf_op jit(solution)/shard_map/all_gather | solution.py:22
  88.2 3.0 fusion.47
  91.2 59.6 %all-to-all-done = bf16[16,96,1536]{2,1,0:T(8,128)(2,1)} async-done(((bf16[16,96,1536]{2,1,0:T(8,128)(2,1)}), bf16[16,96,1536]{2,1,0:T(8,128)(2,1)}, u32[]{:S(2)}, u32[]{:S(2)}) %all-to-all-start) | async-done | bytes 4718624 | tf_op jit(solution)/shard_map/all_to_all | solution.py:17
  150.8 3.8 %fusion.34 = f32[1536,256]{1,0:T(8,128)S(1)} fusion(bf16[1536,1536]{1,0:T(8,128)(2,1)} %bitcast.8, bf16[1,256,1536]{1,2,0:T(8,128)(2,1)S(1)} %all-gather.1), kind=kOutput, calls=%fused_computation.61 | convolution fusion | flops 1207959552 | bytes 7077888 | tf_op jit(solution)/shard_map/dot_general | solution.py:81
  157.3 15.3 %all-gather.5.cloned.1.call-done = bf16[4096,576]{0,1:T(8,128)(2,1)} async-done(((bf16[256,576]{0,1:T(8,128)(2,1)}), bf16[4096,576]{0,1:T(8,128)(2,1)}) %all-gather.5.cloned.1.call-update) | async-done | bytes 4718608 | tf_op jit(solution)/shard_map/all_gather | solution.py:22
  172.6 4.8 %slice.46 = bf16[4096,512]{0,1:T(8,128)(2,1)} slice(bf16[4096,576]{0,1:T(8,128)(2,1)} %all-gather.5.cloned.1.call-done), slice={[0:4096], [0:512]} | slice | bytes 8388608 | tf_op jit(solution)/shard_map/slice | solution.py:24
  177.4 139.5 %while.17 = (s32[]{:T(128)}, f32[8,256]{1,0:T(8,128)S(1)}, f32[8,256]{1,0:T(8,128)S(1)}, f32[8,256,128]{2,1,0:T(8,128)S(1)}, s32[8]{0:T(128)S(1)}, /*index=5*/s3...) while((s32[]{:T(128)}, f32[8,256]{1,0:T(8,128)S(1)}, ...), condition=%wide.region_5.6_spmd.clone, body=%wide.region_1.5_spmd.clone.sunk | while | flops 1757632000 | bytes 48734628 | solution.py:144
  178.7 3.1 gather_fusion
  185.0 3.0 fusion.80
  188.0 3.1 fusion.81
  196.2 3.1 gather_fusion
  205.4 3.1 fusion.81
  213.6 3.1 gather_fusion
  219.9 3.0 fusion.80
  222.8 3.1 fusion.81
  231.1 3.1 gather_fusion
  240.3 3.1 fusion.81
  248.5 3.1 gather_fusion
  254.7 3.0 fusion.80
  257.7 3.1 fusion.81
  265.9 3.1 gather_fusion
  275.1 3.1 fusion.81
  283.4 3.1 gather_fusion
  289.6 3.0 fusion.80
  292.6 3.1 fusion.81
  300.8 3.1 gather_fusion
  310.0 3.1 fusion.81
  317.6 7.2 %all-to-all-start.1 = ((f32[32,1,8]{2,1,0:T(1,128)}), f32[32,1,8]{2,1,0:T(1,128)S(1)}, u32[]{:S(2)}, u32[]{:S(2)}) async-start(f32[32,1,8]{2,1,0:T(1,128)} %broadcast_in_dim.126), calls=%async_computation.1 | async-start | bytes 32768 | tf_op jit(solution)/shard_map/all_to_all | solution.py:31
  326.5 7.6 %all-to-all-done.1 = f32[32,1,8]{2,1,0:T(1,128)S(1)} async-done(((f32[32,1,8]{2,1,0:T(1,128)}), f32[32,1,8]{2,1,0:T(1,128)S(1)}, u32[]{:S(2)}, u32[]{:S(2)}) %all-to-all-start.1) | async-done | bytes 1056 | tf_op jit(solution)/shard_map/all_to_all | solution.py:31
  (214 shorter events, 92.5 us)
Async XLA Ops:
  7.2 8.6 %copy-start.2 = (bf16[96,1536]{1,0:T(8,128)(2,1)S(1)}, bf16[96,1536]{1,0:T(8,128)(2,1)}, u32[]{:S(2)}) copy-start(bf16[96,1536]{1,0:T(8,128)(2,1)} %param.13) | copy-start | bytes 884740
  7.2 81.0 %all-gather.7.cloned.1.call-start = ((), (), s32[]{:S(2)}) async-start(), calls=%async_computation.3 | async-start | bytes 2228224 | tf_op jit(solution)/shard_map/all_gather | solution.py:22
  16.0 2.2 copy-start.3
  18.2 10.2 %copy-start.9 = (s32[1,32]{1,0:T(1,128)S(1)}, s32[1,32]{1,0:T(1,128)}, u32[]{:S(2)}) copy-start(s32[1,32]{1,0:T(1,128)} %param.16) | copy-start | bytes 388
  18.2 10.3 %copy-start.7 = (bf16[1,256,64]{1,2,0:T(8,128)(2,1)S(1)}, bf16[1,256,64]{1,2,0:T(8,128)(2,1)}, u32[]{:S(2)}) copy-start(bf16[1,256,64]{1,2,0:T(8,128)(2,1)} %param.11) | copy-start | bytes 98308
  18.2 35.7 %copy-start.8 = (bf16[1,256,64]{1,2,0:T(8,128)(2,1)S(1)}, bf16[1,256,64]{1,2,0:T(8,128)(2,1)}, u32[]{:S(2)}) copy-start(bf16[1,256,64]{1,2,0:T(8,128)(2,1)} %param.12) | copy-start | bytes 98308
  18.2 36.8 %copy-start = (s32[1,4096]{1,0:T(1,128)S(1)}, s32[1,4096]{1,0:T(1,128)}, u32[]{:S(2)}) copy-start(s32[1,4096]{1,0:T(1,128)} %param.17) | copy-start | bytes 49156
  18.2 38.5 %copy-start.6 = (bf16[1,256,192]{1,2,0:T(8,128)(2,1)S(1)}, bf16[1,256,192]{1,2,0:T(8,128)(2,1)}, u32[]{:S(2)}) copy-start(bf16[1,256,192]{1,2,0:T(8,128)(2,1)} %param.10) | copy-start | bytes 294916
  18.2 132.6 %all-to-all-start = ((bf16[16,96,1536]{2,1,0:T(8,128)(2,1)}), bf16[16,96,1536]{2,1,0:T(8,128)(2,1)}, u32[]{:S(2)}, u32[]{:S(2)}) async-start(bf16[16,96,1536]{2,1,0:T(8,128)(2,1)} %bitcast.84), calls=%async_computation | async-start | bytes 9437184 | tf_op jit(solution)/shard_map/all_to_all | solution.py:17
  28.4 144.2 %all-gather.5.cloned.1.call-start = ((), (), s32[]{:S(2)}) async-start(), calls=%async_computation.2 | async-start | bytes 5013504 | tf_op jit(solution)/shard_map/all_gather | solution.py:22
  154.7 1.2 copy-start.4
  172.6 4.8 %slice-start = ((bf16[4096,576]{0,1:T(8,128)(2,1)}), bf16[4096,64]{0,1:T(8,128)(2,1)S(1)}, s32[]{:S(2)}) async-start(bf16[4096,576]{0,1:T(8,128)(2,1)} %all-gather.5.cloned.1.call-done), calls=%async_computation.4 | async-start | bytes 1048576 | tf_op jit(solution)/shard_map/slice | solution.py:24
  177.3 157.8 %copy-start.5 = (bf16[32,1024]{1,0:T(8,128)(2,1)S(1)}, bf16[32,1024]{1,0:T(8,128)(2,1)}, u32[]{:S(2)}) copy-start(bf16[32,1024]{1,0:T(8,128)(2,1)} %param.14) | copy-start | bytes 196612
  188.0 5.2 %copy-start.1 = (f32[8,256,512]{1,2,0:T(8,128)S(1)}, f32[8,256,512]{1,2,0:T(8,128)}, u32[]{:S(2)}) copy-start(f32[8,256,512]{1,2,0:T(8,128)} %get-tuple-element.455) | copy-start | bytes 12582916 | tf_op jit(solution)/shard_map/while
  205.4 5.2 %copy-start.1 = (f32[8,256,512]{1,2,0:T(8,128)S(1)}, f32[8,256,512]{1,2,0:T(8,128)}, u32[]{:S(2)}) copy-start(f32[8,256,512]{1,2,0:T(8,128)} %get-tuple-element.455) | copy-start | bytes 12582916 | tf_op jit(solution)/shard_map/while
  222.8 5.2 %copy-start.1 = (f32[8,256,512]{1,2,0:T(8,128)S(1)}, f32[8,256,512]{1,2,0:T(8,128)}, u32[]{:S(2)}) copy-start(f32[8,256,512]{1,2,0:T(8,128)} %get-tuple-element.455) | copy-start | bytes 12582916 | tf_op jit(solution)/shard_map/while
  240.3 5.2 %copy-start.1 = (f32[8,256,512]{1,2,0:T(8,128)S(1)}, f32[8,256,512]{1,2,0:T(8,128)}, u32[]{:S(2)}) copy-start(f32[8,256,512]{1,2,0:T(8,128)} %get-tuple-element.455) | copy-start | bytes 12582916 | tf_op jit(solution)/shard_map/while
  257.7 5.2 %copy-start.1 = (f32[8,256,512]{1,2,0:T(8,128)S(1)}, f32[8,256,512]{1,2,0:T(8,128)}, u32[]{:S(2)}) copy-start(f32[8,256,512]{1,2,0:T(8,128)} %get-tuple-element.455) | copy-start | bytes 12582916 | tf_op jit(solution)/shard_map/while
  275.1 5.2 %copy-start.1 = (f32[8,256,512]{1,2,0:T(8,128)S(1)}, f32[8,256,512]{1,2,0:T(8,128)}, u32[]{:S(2)}) copy-start(f32[8,256,512]{1,2,0:T(8,128)} %get-tuple-element.455) | copy-start | bytes 12582916 | tf_op jit(solution)/shard_map/while
  292.6 5.2 %copy-start.1 = (f32[8,256,512]{1,2,0:T(8,128)S(1)}, f32[8,256,512]{1,2,0:T(8,128)}, u32[]{:S(2)}) copy-start(f32[8,256,512]{1,2,0:T(8,128)} %get-tuple-element.455) | copy-start | bytes 12582916 | tf_op jit(solution)/shard_map/while
  310.0 5.2 %copy-start.1 = (f32[8,256,512]{1,2,0:T(8,128)S(1)}, f32[8,256,512]{1,2,0:T(8,128)}, u32[]{:S(2)}) copy-start(f32[8,256,512]{1,2,0:T(8,128)} %get-tuple-element.455) | copy-start | bytes 12582916 | tf_op jit(solution)/shard_map/while
  317.6 16.5 %all-to-all-start.1 = ((f32[32,1,8]{2,1,0:T(1,128)}), f32[32,1,8]{2,1,0:T(1,128)S(1)}, u32[]{:S(2)}, u32[]{:S(2)}) async-start(f32[32,1,8]{2,1,0:T(1,128)} %broadcast_in_dim.126), calls=%async_computation.1 | async-start | bytes 32768 | tf_op jit(solution)/shard_map/all_to_all | solution.py:31
Sparse Core Ops, SparseCore 0:
  10.4 77.7 all-gather.6
  90.5 82.0 all-gather.4
